TPU v7x, 512 devices: a whole 4x8x8 slice. The times are simulated.
512 devices in a mesh: trial: 4 (over x), span: 16 (over y, core), heads: 8 (over z).
Axes of the slice: x: 4, y: 8, z: 8, core: 2. Of those that a mesh axis runs over, the one named last changes fastest.
Arguments:
- latents: bfloat16 [64, 4096, 512], P('trial', ('span', 'heads')), parts along dimension 0, may hold values from -6 to 6
- rotary_rows: bfloat16 [64, 4096, 64], P('trial', ('span', 'heads')), parts along dimension 0, may hold values from -6 to 6
- latent_gain: float32 [512], replicated, may hold values from 0.25 to 1.75
- key_up: bfloat16 [2048, 16, 128], P('trial', 'heads'), parts along dimension 0, may hold values from -0.25 to 0.25
- value_up: bfloat16 [2048, 16, 128], P('trial', 'heads'), parts along dimension 0, may hold values from -0.25 to 0.25
Outputs:
- cache_keys: bfloat16 [64, 16, 192, 4096], P(('trial', 'span'), 'heads'), parts along dimension 0
- cache_values: bfloat16 [64, 4096, 16, 128], P(('trial', 'span'), None, 'heads'), parts along dimension 0
There are 4 independent parts, one for each index of `trial`. A program takes and returns all parts, laid end to end along the dimension named above; an argument that names none is the same for every part. Nothing has to cross between parts.
All inputs are finite; a program needn't handle non-finite values.
Results may differ from a plain program's by a relative error of at most 0.0049.
Values may be sent and summed in bfloat16 or wider, within the bound.
A program may use at most 64 MiB of HBM per device.

v0:
```python
import jax
import jax.numpy as jnp
from jax import lax
from jax.sharding import PartitionSpec as P


def in_one_piece(arrays, axis, split_dim, concat_dim, along):
    ends, at = ([], 0)
    for a in arrays[:-1]:
        at += a.shape[along]
        ends.append(at)
    both = jnp.concatenate(arrays, axis=along)
    return tuple(
        jnp.split(
            lax.all_to_all(both, axis, split_axis=split_dim, concat_axis=concat_dim, tiled=True),
            ends,
            axis=along,
        )
    )


def widen_rows(rows, rotary, key_up, value_up):
    wide_keys = jnp.einsum(
        "btr,rhk->bthk", rows, key_up, preferred_element_type=jnp.float32
    ).astype(jnp.bfloat16)
    shared = jnp.broadcast_to(rotary[:, :, None], wide_keys.shape[:3] + rotary.shape[2:])
    wide_values = jnp.einsum(
        "btr,rhk->bthk", rows, value_up, preferred_element_type=jnp.float32
    ).astype(jnp.bfloat16)
    return (jnp.concatenate([wide_keys, shared], axis=-1), wide_values)


def unit_rows(vectors, row_gain):
    return (
        vectors * lax.rsqrt(jnp.mean(vectors * vectors, axis=-1, keepdims=True) + 1e-06) * row_gain
    )


def shards(latents, rotary_rows, latent_gain, key_up, value_up):
    rows_ready = unit_rows(latents.astype(jnp.float32), latent_gain).astype(jnp.bfloat16)
    rows_moved, rotary_moved = in_one_piece((rows_ready, rotary_rows), "span", 0, 1, 2)
    rows_cut = rows_moved.reshape(
        rows_moved.shape[0], lax.axis_size("span"), -1, rows_moved.shape[2]
    )
    rotary_cut = rotary_moved.reshape(
        rotary_moved.shape[0], lax.axis_size("span"), -1, rotary_moved.shape[2]
    )
    rows_joined, rotary_joined = (
        lax.all_gather(rows_cut, "heads", axis=2, tiled=True),
        lax.all_gather(rotary_cut, "heads", axis=2, tiled=True),
    )
    rows_whole = rows_joined.reshape(rows_joined.shape[0], -1, rows_joined.shape[3])
    rotary_whole = rotary_joined.reshape(rotary_joined.shape[0], -1, rotary_joined.shape[3])
    cache_keys, cache_values = widen_rows(rows_whole, rotary_whole, key_up, value_up)
    cache_keys = jnp.transpose(cache_keys, (0, 2, 3, 1))
    return (cache_keys, cache_values)


def solution(mesh):
    return jax.shard_map(
        shards,
        mesh=mesh,
        in_specs=(
            P("trial", ("span", "heads"), None),
            P("trial", ("span", "heads"), None),
            P(),
            P("trial", "heads", None),
            P("trial", "heads", None),
        ),
        out_specs=(
            P(("trial", "span"), "heads", None, None),
            P(("trial", "span"), None, "heads", None),
        ),
        check_vma=False,
    )
```

profile of v0, /device:TPU:6, one launch (start us, length us, event | category | flops | bytes accessed | tf_op | source)
XLA Modules:
  0.0 137.5 jit_solution(17999335200704216173)
XLA Ops:
  7.2 0.0 copy-start
  7.2 0.0 copy-start.2
  7.2 0.0 all-gather.2.cloned.1.call-start
  7.2 1.3 fusion.1
  8.5 1.2 fusion.3
  9.8 1.0 pad_maximum_fusion
  10.7 27.0 %all_to_all.12 = bf16[16,32,576]{2,1,0:T(8,128)(2,1)S(1)} all-to-all(bf16[16,32,576]{2,1,0:T(8,128)(2,1)S(1)} %pad_maximum_fusion), channel_id=1, replica_groups=mesh['trial'=4,'span'=16,'heads'=8] {'span'}, dimensions={0} | all-to-all | bytes 1179648 | tf_op jit(solution)/shard_map/all_to_all | solution.py:15
  37.7 0.8 split.8
  38.5 0.0 all-gather.2.cloned.1.call-update
  38.6 0.0 copy-done.2
  38.6 0.2 copy.14
  38.8 0.1 copy.15
  38.8 36.3 %all_gather.7 = bf16[1,16,256,64]{3,1,0,2:T(8,128)(2,1)S(1)} all-gather(bf16[1,16,32,64]{3,1,0,2:T(8,128)(2,1)S(1)} %copy.15), channel_id=1, replica_groups=mesh['trial'=4,'span'=16,'heads'=8] {'heads'}, dimensions={2}, use_global_device_ids=true | all-gather | bytes 589824 | tf_op jit(solution)/shard_map/all_gather | solution.py:50
  75.1 1.3 copy.16
  76.5 0.2 copy.19
  76.7 27.0 %all-gather.2.cloned.1.call-done = bf16[1,16,256,512]{3,2,1,0:T(8,128)(2,1)} async-done(((bf16[1,16,32,512]{3,2,1,0:T(8,128)(2,1)}), bf16[1,16,256,512]{3,2,1,0:T(8,128)(2,1)}) %all-gather.2.cloned.1.call-update) | async-done | bytes 4194320 | tf_op jit(solution)/shard_map/all_gather | solution.py:49
  103.7 3.5 %fusion.5 = f32[4096,256]{0,1:S(1)} fusion(bf16[4096,512]{1,0:T(8,128)(2,1)} %bitcast.23, bf16[512,256]{0,1:T(8,128)(2,1)S(1)} %bitcast.30), kind=kOutput, calls=%fused_computation.12 | convolution fusion | flops 1073741824 | bytes 8650752
  107.1 0.0 copy-start.1
  107.1 0.3 convert_bitcast_fusion
  107.4 0.0 copy-done
  107.4 1.9 %copy-done.1 = bf16[1,16,256,512]{3,2,1,0:T(8,128)(2,1)S(1)} copy-done((bf16[1,16,256,512]{3,2,1,0:T(8,128)(2,1)S(1)}, bf16[1,16,256,512]{3,2,1,0:T(8,128)(2,1)}, u32[]{:S(2)}) %copy-start.1) | copy-done | bytes 4194328
  109.3 1.3 fusion
  110.6 18.1 %copy.18 = bf16[1,4096,2,128]{3,2,1,0:T(2,128)(2,1)} copy(bf16[1,4096,2,128]{3,1,2,0:T(8,128)(2,1)S(1)} %fusion) | data formatting | bytes 4194304
  128.7 0.1 broadcast_in_dim.10
  128.8 1.9 %maximum_bitcast_fusion = bf16[1,2,192,4096]{3,2,1,0:T(8,128)(2,1)} fusion(bf16[1,4096,2,64]{1,3,2,0:T(8,128)(2,1)S(1)} %broadcast_in_dim.10, bf16[1,4096,2,128]{1,3,2,0:T(8,128)(2,1)S(1)} %convert_bitcast_fusion), kind=kLoop, calls=%fused_computation.2 | loop fusion | flops 6291456 | bytes 6291456 | tf_op jit(solution)/shard_map/transpose | solution.py:55
  (2 shorter events, 0.0 us)
Async XLA Ops:
  7.2 100.3 %copy-start = (bf16[512,2,128]{2,1,0:T(2,128)(2,1)S(1)}, bf16[512,2,128]{2,1,0:T(2,128)(2,1)}, u32[]{:S(2)}) copy-start(bf16[512,2,128]{2,1,0:T(2,128)(2,1)} %param.9) | copy-start | bytes 786436
  7.2 31.4 %copy-start.2 = (bf16[512,2,128]{2,1,0:T(2,128)(2,1)S(1)}, bf16[512,2,128]{2,1,0:T(2,128)(2,1)}, u32[]{:S(2)}) copy-start(bf16[512,2,128]{2,1,0:T(2,128)(2,1)} %param.8) | copy-start | bytes 786436
  7.2 96.5 %all-gather.2.cloned.1.call-start = ((), (), s32[]{:S(2)}) async-start(), calls=%async_computation.1 | async-start | bytes 4718592 | tf_op jit(solution)/shard_map/all_gather | solution.py:49
  107.1 2.2 %copy-start.1 = (bf16[1,16,256,512]{3,2,1,0:T(8,128)(2,1)S(1)}, bf16[1,16,256,512]{3,2,1,0:T(8,128)(2,1)}, u32[]{:S(2)}) copy-start(bf16[1,16,256,512]{3,2,1,0:T(8,128)(2,1)} %all-gather.2.cloned.1.call-done) | copy-start | bytes 12582916
Sparse Core Ops, SparseCore 0:
  38.7 64.9 all-gather.1
where the time goes:
time: 139 us; the launch traced here: 138 us
  blocking collectives  63.3 us (46%)
  waiting for transfers between devices  27 us (19%)
  local copies, waits for them, and re-layouts  22.7 us (16%)
  between operations  14.2 us (10%)
  other arithmetic  5.63 us (4%)
  matrix products  4.72 us (3%)
    all_gather x1, blocking collectives, shards(): lax.all_gather(rotary_cut, 'heads', axis=2, tiled=True)  36.3 us
    all_gather x1, waiting for transfers between devices, shards(): lax.all_gather(rows_cut, 'heads', axis=2, tiled=True)  27 us
    all_to_all x1, blocking collectives, in_one_piece(): lax.all_to_all(both, axis, split_axis=split_dim, concat_axis=concat_dim,...  27 us
    unnamed x9, local copies, waits for them, and re-layouts  20.4 us
    unnamed x1, matrix products  3.47 us
  transfers between devices with their start and end apart: 1, of which 1 were waited for; matrix products, arithmetic and copies ran while one was open for 1% of the time, Pallas kernels for 0%

commit v1 on v0

v1 whole, which is shorter than its diff:
```python
import jax
import jax.numpy as jnp
from jax import lax
from jax.experimental import pallas as pl
from jax.experimental.pallas import tpu as pltpu
from jax.sharding import PartitionSpec as P

MESH = pl.DeviceIdType.MESH
SPAN = 16
RING = 8
ROWS = 32
LATENT = 512
ROTARY = 64
PART = 128
CHUNK = 144
GROUP = 4
TILE = RING * ROWS


def source_of(j, span):
    i = j // 2
    odd = i % 2
    dy = odd * ((i + 1) // 2) + (1 - odd) * (8 - i // 2)
    y, core = span // 2, span % 2
    swap = j % 2
    other = core + swap - 2 * core * swap
    return ((y + dy) % 8) * 2 + other


def target_of(j, span):
    i = j // 2
    odd = i % 2
    dy = odd * ((i + 1) // 2) + (1 - odd) * (8 - i // 2)
    y, core = span // 2, span % 2
    swap = j % 2
    other = core + swap - 2 * core * swap
    return ((y + 8 - dy) % 8) * 2 + other


def kernel(
    lat_hbm, rot_hbm, gain_hbm, wk_hbm, wv_hbm,
    keys_hbm, values_hbm,
    lat, rot, gain, wk_pairs, wv_pairs, wide, wk, wv,
    ready, held, kst, vwide, vst,
    in_sem, swap_send, swap_recv, up_send, up_recv, down_send, down_recv, out_sem,
):
    span, z = lax.axis_index("span"), lax.axis_index("heads")
    up, down = (z + 1) % RING, (z + RING - 1) % RING

    barrier = pltpu.get_barrier_semaphore()
    for j in range(1, SPAN):
        pl.semaphore_signal(barrier, inc=1, device_id={"span": target_of(j, span)}, device_id_type=MESH)
    for peer in (up, down):
        pl.semaphore_signal(barrier, inc=1, device_id={"heads": peer}, device_id_type=MESH)

    loads = [
        pltpu.make_async_copy(src, dst, in_sem.at[n])
        for n, (src, dst) in enumerate(
            ((lat_hbm, lat), (gain_hbm, gain), (rot_hbm, rot), (wk_hbm, wk_pairs), (wv_hbm, wv_pairs))
        )
    ]
    for load in loads:
        load.start()
    for load in loads[:3]:
        load.wait()

    def make_ready(s, carry):
        x = lat[s].astype(jnp.float32)
        x = x * lax.rsqrt(jnp.mean(x * x, axis=-1, keepdims=True) + 1e-06) * gain[...]
        x = x.astype(jnp.bfloat16)
        for q in range(4):
            ready[s, pl.ds(q * ROWS, ROWS), :] = x[:, q * 128 : (q + 1) * 128]
        r = rot[s]
        ready[s, pl.ds(4 * ROWS, 16), :] = jnp.concatenate([r[:16], r[16:]], axis=1)
        return carry

    lax.fori_loop(0, SPAN, make_ready, 0, unroll=4)
    held[0, z] = ready[span]

    pl.semaphore_wait(barrier, SPAN - 1 + 2)

    def swap(j):
        target = target_of(j, span)
        return pltpu.make_async_remote_copy(
            src_ref=ready.at[target],
            dst_ref=held.at[j, z],
            send_sem=swap_send,
            recv_sem=swap_recv.at[j],
            device_id={"span": target},
            device_id_type=MESH,
        )

    def upward(j, k):
        owner = (z + RING - k) % RING
        return pltpu.make_async_remote_copy(
            src_ref=held.at[j, owner],
            dst_ref=held.at[j, owner],
            send_sem=up_send,
            recv_sem=up_recv.at[j, k],
            device_id={"heads": up},
            device_id_type=MESH,
        )

    def downward(j, k):
        owner = (z + k) % RING
        return pltpu.make_async_remote_copy(
            src_ref=held.at[j, owner],
            dst_ref=held.at[j, owner],
            send_sem=down_send,
            recv_sem=down_recv.at[j, k],
            device_id={"heads": down},
            device_id_type=MESH,
        )

    def send_step(g, k):
        for m in range(GROUP):
            j = g * GROUP + m
            if k == 0:
                @pl.when(j > 0)
                def _():
                    swap(j).wait_recv()
            if k < 3 or m < 2:
                if k > 0:
                    upward(j, k - 1).wait_recv()
                upward(j, k).start()
            if k < 3 or m >= 2:
                if k > 0:
                    downward(j, k - 1).wait_recv()
                downward(j, k).start()

    def finish(g, m):
        j = g * GROUP + m
        upward(j, 3 if m < 2 else 2).wait_recv()
        downward(j, 2 if m < 2 else 3).wait_recv()
        rows = jnp.concatenate(
            [held[j, :, pl.ds(q * ROWS, ROWS), :].reshape(TILE, 128) for q in range(4)], axis=1
        )
        keys = lax.dot_general(
            wk[...], rows, (((1,), (1,)), ((), ())), preferred_element_type=jnp.float32
        ).astype(jnp.bfloat16)
        turned = held[j, :, pl.ds(4 * ROWS, 16), :].astype(jnp.float32)
        turned = jnp.concatenate([turned[:, :, :ROTARY], turned[:, :, ROTARY:]], axis=1)
        turned = turned.reshape(TILE, ROTARY).T.astype(jnp.bfloat16)
        values = jnp.dot(rows, wv[...], preferred_element_type=jnp.float32)
        for h in range(2):
            kst[j, h, pl.ds(0, PART), :] = keys[h * PART : (h + 1) * PART]
            kst[j, h, pl.ds(PART, ROTARY), :] = turned
            vwide[pl.ds(h, TILE, stride=2), :] = values[:, h * PART : (h + 1) * PART]
        vst[j] = vwide[...].astype(jnp.bfloat16)
        source = source_of(j, span)
        pltpu.make_async_copy(
            kst.at[j], keys_hbm.at[:, :, pl.ds(pl.multiple_of(source * TILE, TILE), TILE)], out_sem.at[0]
        ).start()
        pltpu.make_async_copy(
            vst.at[j], values_hbm.at[pl.ds(pl.multiple_of(source * 2 * TILE, 2 * TILE), 2 * TILE), :], out_sem.at[1]
        ).start()

    for j in range(1, SPAN):
        swap(j).start()

    for load in loads[3:]:
        load.wait()
    wide[...] = wk_pairs[...].astype(jnp.float32)
    for h in range(2):
        wk[pl.ds(h * PART, PART), :] = wide[pl.ds(h, LATENT, stride=2), :].T.astype(jnp.bfloat16)
    wide[...] = wv_pairs[...].astype(jnp.float32)
    for h in range(2):
        wv[:, pl.ds(h * PART, PART)] = wide[pl.ds(h, LATENT, stride=2), :].astype(jnp.bfloat16)

    def group(g, carry):
        send_step(g, 0)
        send_step(g, 1)

        @pl.when(g > 0)
        def _():
            finish(g - 1, 0)
            finish(g - 1, 1)

        send_step(g, 2)

        @pl.when(g > 0)
        def _():
            finish(g - 1, 2)
            finish(g - 1, 3)

        send_step(g, 3)
        return carry

    lax.fori_loop(0, SPAN // GROUP, group, 0)
    for m in (0, 2, 1, 3):
        finish(SPAN // GROUP - 1, m)

    def all_of(ref, sem):
        pltpu.make_async_copy(ref, ref, sem).wait()

    all_of(ready.at[pl.ds(0, SPAN - 1)], swap_send)
    all_of(held.at[pl.ds(0, 7)], up_send)
    all_of(held.at[pl.ds(0, 7)], down_send)
    all_of(kst, out_sem.at[0])
    all_of(vst, out_sem.at[1])


def shards(latents, rotary_rows, latent_gain, key_up, value_up):
    anywhere = pl.BlockSpec(memory_space=pl.ANY)
    keys, values = pl.pallas_call(
        kernel,
        out_shape=(
            jax.ShapeDtypeStruct((2, PART + ROTARY, SPAN * TILE), jnp.bfloat16),
            jax.ShapeDtypeStruct((SPAN * TILE * 2, PART), jnp.bfloat16),
        ),
        in_specs=[anywhere] * 5,
        out_specs=(anywhere, anywhere),
        scratch_shapes=[
            pltpu.VMEM((SPAN, ROWS, LATENT), jnp.bfloat16),
            pltpu.VMEM((SPAN, ROWS, ROTARY), jnp.bfloat16),
            pltpu.VMEM((1, LATENT), jnp.float32),
            pltpu.VMEM((2 * LATENT, PART), jnp.bfloat16),
            pltpu.VMEM((2 * LATENT, PART), jnp.bfloat16),
            pltpu.VMEM((2 * LATENT, PART), jnp.float32),
            pltpu.VMEM((2 * PART, LATENT), jnp.bfloat16),
            pltpu.VMEM((LATENT, 2 * PART), jnp.bfloat16),
            pltpu.VMEM((SPAN, CHUNK, 128), jnp.bfloat16),
            pltpu.VMEM((SPAN, RING, CHUNK, 128), jnp.bfloat16),
            pltpu.VMEM((SPAN, 2, PART + ROTARY, TILE), jnp.bfloat16),
            pltpu.VMEM((2 * TILE, PART), jnp.float32),
            pltpu.VMEM((SPAN, 2 * TILE, PART), jnp.bfloat16),
            pltpu.SemaphoreType.DMA((5,)),
            pltpu.SemaphoreType.DMA,
            pltpu.SemaphoreType.DMA((SPAN,)),
            pltpu.SemaphoreType.DMA,
            pltpu.SemaphoreType.DMA((SPAN, 4)),
            pltpu.SemaphoreType.DMA,
            pltpu.SemaphoreType.DMA((SPAN, 4)),
            pltpu.SemaphoreType.DMA((2,)),
        ],
        compiler_params=pltpu.CompilerParams(collective_id=0, has_side_effects=True),
    )(
        latents,
        rotary_rows,
        latent_gain.reshape(1, LATENT),
        key_up.reshape(2 * LATENT, PART),
        value_up.reshape(2 * LATENT, PART),
    )
    return keys[None], values.reshape(1, SPAN * TILE, 2, PART)


def solution(mesh):
    return jax.shard_map(
        shards,
        mesh=mesh,
        in_specs=(
            P("trial", ("span", "heads"), None),
            P("trial", ("span", "heads"), None),
            P(),
            P("trial", "heads", None),
            P("trial", "heads", None),
        ),
        out_specs=(
            P(("trial", "span"), "heads", None, None),
            P(("trial", "span"), None, "heads", None),
        ),
        check_vma=False,
    )
```

time: 139 us -> 79.3 us (0.57)
  Pallas kernels: 0 us -> 73.1 us
  blocking collectives: 63.3 us -> 0 us
  waiting for transfers between devices: 27 us -> 0 us
  local copies, waits for them, and re-layouts: 22.7 us -> 5.38 us
  between operations: 14.2 us -> 0.65 us
  other arithmetic: 5.63 us -> 0 us
  matrix products: 4.72 us -> 0 us
    pallas_call x0 -> x1, Pallas kernels: none -> 73.1 us  [shards(): pl.pallas_call(kernel, out_shape=(jax.ShapeDtypeStruct((2, PART + ROTARY,...]
    all_gather x1 -> x0, blocking collectives: 36.3 us -> none  [shards(): lax.all_gather(rotary_cut, 'heads', axis=2, tiled=True)]
    all_gather x1 -> x0, waiting for transfers between devices: 27 us -> none  [shards(): lax.all_gather(rows_cut, 'heads', axis=2, tiled=True)]
    all_to_all x1 -> x0, blocking collectives: 27 us -> none  [in_one_piece(): lax.all_to_all(both, axis, split_axis=split_dim, concat_axis=concat_dim,...]
    unnamed x9 -> x4, local copies, waits for them, and re-layouts: 20.4 us -> 5.38 us
    unnamed x1 -> x0, matrix products: 3.47 us -> none
    transpose x1 -> x0, other arithmetic: 1.87 us -> none  [shards(): cache_keys = jnp.transpose(cache_keys, (0, 2, 3, 1))]
    convert_element_type x2 -> x0, other arithmetic: 1.51 us -> none  [the longest x1 1.23 us: shards(): unit_rows(latents.astype(jnp.float32), latent_gain).astype(jnp.bfloat16)]
  transfers between devices with their start and end apart: 1 -> 0, of which waited for: 1 -> 0; matrix products, arithmetic and copies ran while one was open for 1% -> 0% of each run, Pallas kernels for 0% -> 0%
where the time goes in v1:
time: 79.3 us; the launch traced here: 79.2 us
  Pallas kernels  73.1 us (92%)
  local copies, waits for them, and re-layouts  5.38 us (7%)
    pallas_call x1, Pallas kernels, shards(): pl.pallas_call(kernel, out_shape=(jax.ShapeDtypeStruct((2, PART + ROTARY,...  73.1 us
    unnamed x4, local copies, waits for them, and re-layouts  5.38 us

profile of v1, /device:TPU:6, one launch (start us, length us, event | category | flops | bytes accessed | tf_op | source)
XLA Modules:
  0.0 79.2 jit_solution(12160959527627098984)
XLA Ops:
  0.6 73.1 %shard_map.68 = (bf16[2,192,4096]{2,1,0:T(8,128)(2,1)}, bf16[8192,128]{1,0:T(8,128)(2,1)}) custom-call(bf16[16,32,512]{2,1,0:T(8,128)(2,1)} %lat_hbm.1, bf16[16,32,64]{2,1,0:T(8,128)(2,1)} %rot_hbm.1, f32[1,512]{1,0:T(1,128)} %bitcast.9, bf16[1024,128]{1,0:T(8,128)(2,1)} %bitcast.7, bf16[1024,128]{1,0:T(8,128)(2,1)} %bitcast.8), custom_call_target="tpu_custom_call" | custom-call | tf_op jit(solution)/shard_map/pallas_call | solution.py:205
  73.8 0.0 copy-start
  73.8 4.1 %copy.9 = bf16[1,2,192,4096]{3,2,1,0:T(8,128)(2,1)} copy(bf16[1,2,192,4096]{3,2,1,0:T(8,128)(2,1)} %bitcast.5) | data formatting | bytes 6291456
  77.8 0.0 copy-done
  77.8 1.3 %copy.10 = bf16[1,4096,2,128]{3,2,1,0:T(2,128)(2,1)} copy(bf16[1,4096,2,128]{3,2,1,0:T(2,128)(2,1)S(1)} %bitcast.6) | data formatting | bytes 4194304
Async XLA Ops:
  73.8 4.1 %copy-start = (bf16[8192,128]{1,0:T(8,128)(2,1)S(1)}, bf16[8192,128]{1,0:T(8,128)(2,1)}, u32[]{:S(2)}) copy-start(bf16[8192,128]{1,0:T(8,128)(2,1)} %get-tuple-element.5) | copy-start | bytes 6291460

commit v2 on v1

v2 whole, which is shorter than its diff:
```python
import jax
import jax.numpy as jnp
from jax import lax
from jax.experimental import pallas as pl
from jax.experimental.pallas import tpu as pltpu
from jax.sharding import PartitionSpec as P

MESH = pl.DeviceIdType.MESH
SPAN = 16
RING = 8
ROWS = 32
LATENT = 512
ROTARY = 64
PART = 128
CHUNK = 144
GROUP = 8
TILE = RING * ROWS


def source_of(j, span):
    i = j // 2
    odd = i % 2
    dy = odd * ((i + 1) // 2) + (1 - odd) * (8 - i // 2)
    y, core = span // 2, span % 2
    swap = j % 2
    other = core + swap - 2 * core * swap
    return ((y + dy) % 8) * 2 + other


def target_of(j, span):
    i = j // 2
    odd = i % 2
    dy = odd * ((i + 1) // 2) + (1 - odd) * (8 - i // 2)
    y, core = span // 2, span % 2
    swap = j % 2
    other = core + swap - 2 * core * swap
    return ((y + 8 - dy) % 8) * 2 + other


def schedule():
    half = GROUP // 2
    order = [m // 2 + half * (m % 2) for m in range(GROUP)]
    events, owed = [], []
    for first in range(0, SPAN, GROUP):
        for step in range(4):
            for m in range(GROUP):
                if step < 3 or m < half:
                    events.append(("up", first + m, step))
                if step < 3 or m >= half:
                    events.append(("down", first + m, step))
            events += [("finish", j, 0) for j in owed[:half]]
            owed = owed[half:]
        owed = [first + m for m in order]
    return events + [("finish", j, 0) for j in owed]


def gather_kernel(
    lat_hbm, rot_hbm, gain_hbm, wk_hbm, wv_hbm,
    kst, vst,
    own_lat, lat, rot, gain, wk_pairs, wv_pairs, wide, wk, wv, ready, held, vwide,
    in_sem, swap_send, swap_recv, up_send, up_recv, down_send, down_recv,
):
    span, z = lax.axis_index("span"), lax.axis_index("heads")
    up, down = (z + 1) % RING, (z + RING - 1) % RING
    half = GROUP // 2

    barrier = pltpu.get_barrier_semaphore()
    for peer in (up, down):
        pl.semaphore_signal(barrier, inc=1, device_id={"heads": peer}, device_id_type=MESH)
    for j in range(1, SPAN):
        pl.semaphore_signal(barrier, inc=1, device_id={"span": target_of(j, span)}, device_id_type=MESH)

    loads = [
        pltpu.make_async_copy(source, into, in_sem.at[n])
        for n, (source, into) in enumerate(
            (
                (lat_hbm.at[span], own_lat), (gain_hbm, gain), (rot_hbm, rot),
                (lat_hbm, lat), (wk_hbm, wk_pairs), (wv_hbm, wv_pairs),
            )
        )
    ]
    for load in loads:
        load.start()

    def packed(x, r, store):
        x = x.astype(jnp.float32)
        x = x * lax.rsqrt(jnp.mean(x * x, axis=-1, keepdims=True) + 1e-06) * gain[...]
        x = x.astype(jnp.bfloat16)
        for q in range(4):
            store(pl.ds(q * ROWS, ROWS), x[:, q * 128 : (q + 1) * 128])
        store(pl.ds(4 * ROWS, 16), jnp.concatenate([r[:16], r[16:]], axis=1))

    def swap(j):
        return pltpu.make_async_remote_copy(
            src_ref=ready.at[j],
            dst_ref=held.at[j, z],
            send_sem=swap_send,
            recv_sem=swap_recv.at[j],
            device_id={"span": target_of(j, span)},
            device_id_type=MESH,
        )

    def hop(way, j, k):
        owner = (z + RING - k) % RING if way == "up" else (z + k) % RING
        return pltpu.make_async_remote_copy(
            src_ref=held.at[j, owner],
            dst_ref=held.at[j, owner],
            send_sem=up_send if way == "up" else down_send,
            recv_sem=(up_recv if way == "up" else down_recv).at[j, k],
            device_id={"heads": up if way == "up" else down},
            device_id_type=MESH,
        )

    def finish(j):
        rows = jnp.concatenate(
            [held[j, :, pl.ds(q * ROWS, ROWS), :].reshape(TILE, 128) for q in range(4)], axis=1
        )
        keys = lax.dot_general(
            wk[...], rows, (((1,), (1,)), ((), ())), preferred_element_type=jnp.float32
        ).astype(jnp.bfloat16)
        turned = held[j, :, pl.ds(4 * ROWS, 16), :].astype(jnp.float32)
        turned = jnp.concatenate([turned[:, :, :ROTARY], turned[:, :, ROTARY:]], axis=1)
        turned = turned.reshape(TILE, ROTARY).T.astype(jnp.bfloat16)
        values = jnp.dot(rows, wv[...], preferred_element_type=jnp.float32)
        for h in range(2):
            kst[j, h, pl.ds(0, PART), :] = keys[h * PART : (h + 1) * PART]
            kst[j, h, pl.ds(PART, ROTARY), :] = turned
            vwide[pl.ds(h, TILE, stride=2), :] = values[:, h * PART : (h + 1) * PART]
        vst[j] = vwide[...].astype(jnp.bfloat16)

    def store_own(at, x):
        held[0, z, at, :] = x

    def prepare(j):
        target = target_of(j, span)

        def store(at, x):
            ready[j, at, :] = x

        packed(lat[target], rot[target], store)

    for load in loads[:3]:
        load.wait()
    packed(own_lat[...], rot[span], store_own)
    loads[3].wait()
    prepare(1)
    pl.semaphore_wait(barrier, SPAN - 1 + 2)
    hop("up", 0, 0).start()
    hop("down", 0, 0).start()
    for j in range(1, SPAN):
        if j + 1 < SPAN:
            prepare(j + 1)
        swap(j).start()

    arrived = set()

    def arrive(kind, j, k):
        if (kind, j, k) not in arrived:
            arrived.add((kind, j, k))
            if kind == "swap":
                swap(j).wait_recv()
            else:
                hop(kind, j, k).wait_recv()

    weighed = False
    for kind, j, k in schedule():
        if kind == "finish":
            if not weighed:
                weighed = True
                for load in loads[4:]:
                    load.wait()
                wide[...] = wk_pairs[...].astype(jnp.float32)
                for h in range(2):
                    wk[pl.ds(h * PART, PART), :] = wide[pl.ds(h, LATENT, stride=2), :].T.astype(jnp.bfloat16)
                wide[...] = wv_pairs[...].astype(jnp.float32)
                for h in range(2):
                    wv[:, pl.ds(h * PART, PART)] = wide[pl.ds(h, LATENT, stride=2), :].astype(jnp.bfloat16)
            last_up = 3 if j % GROUP < half else 2
            arrive("up", j, last_up)
            arrive("down", j, 5 - last_up)
            finish(j)
        elif (j, k) != (0, 0):
            if k > 0:
                arrive(kind, j, k - 1)
            else:
                arrive("swap", j, 0)
            hop(kind, j, k).start()

    def all_of(ref, sem):
        pltpu.make_async_copy(ref, ref, sem).wait()

    all_of(ready.at[pl.ds(1, SPAN - 1)], swap_send)
    all_of(held.at[pl.ds(0, 7)], up_send)
    all_of(held.at[pl.ds(0, 7)], down_send)


def write_kernel(kst, vst, keys_hbm, values_hbm, sem):
    span = lax.axis_index("span")
    for j in range(SPAN):
        at = source_of(j, span) * TILE
        pltpu.make_async_copy(kst.at[j], keys_hbm.at[:, :, pl.ds(pl.multiple_of(at, TILE), TILE)], sem.at[0]).start()
        pltpu.make_async_copy(
            vst.at[j], values_hbm.at[pl.ds(pl.multiple_of(2 * at, 2 * TILE), 2 * TILE), :], sem.at[1]
        ).start()
    pltpu.make_async_copy(kst, kst, sem.at[0]).wait()
    pltpu.make_async_copy(vst, vst, sem.at[1]).wait()


def shards(latents, rotary_rows, latent_gain, key_up, value_up):
    anywhere = pl.BlockSpec(memory_space=pl.ANY)
    here = pl.BlockSpec(memory_space=pltpu.VMEM)
    kst, vst = pl.pallas_call(
        gather_kernel,
        out_shape=(
            pltpu.VMEM((SPAN, 2, PART + ROTARY, TILE), jnp.bfloat16),
            pltpu.VMEM((SPAN, 2 * TILE, PART), jnp.bfloat16),
        ),
        in_specs=[pl.BlockSpec(memory_space=pltpu.HBM)] * 5,
        out_specs=(here, here),
        scratch_shapes=[
            pltpu.VMEM((ROWS, LATENT), jnp.bfloat16),
            pltpu.VMEM((SPAN, ROWS, LATENT), jnp.bfloat16),
            pltpu.VMEM((SPAN, ROWS, ROTARY), jnp.bfloat16),
            pltpu.VMEM((1, LATENT), jnp.float32),
            pltpu.VMEM((2 * LATENT, PART), jnp.bfloat16),
            pltpu.VMEM((2 * LATENT, PART), jnp.bfloat16),
            pltpu.VMEM((2 * LATENT, PART), jnp.float32),
            pltpu.VMEM((2 * PART, LATENT), jnp.bfloat16),
            pltpu.VMEM((LATENT, 2 * PART), jnp.bfloat16),
            pltpu.VMEM((SPAN, CHUNK, 128), jnp.bfloat16),
            pltpu.VMEM((SPAN, RING, CHUNK, 128), jnp.bfloat16),
            pltpu.VMEM((2 * TILE, PART), jnp.float32),
            pltpu.SemaphoreType.DMA((6,)),
            pltpu.SemaphoreType.DMA,
            pltpu.SemaphoreType.DMA((SPAN,)),
            pltpu.SemaphoreType.DMA,
            pltpu.SemaphoreType.DMA((SPAN, 4)),
            pltpu.SemaphoreType.DMA,
            pltpu.SemaphoreType.DMA((SPAN, 4)),
        ],
        compiler_params=pltpu.CompilerParams(
            collective_id=0, has_side_effects=True, vmem_limit_bytes=24 * 2**20
        ),
    )(
        *(
            pltpu.with_memory_space_constraint(x, pltpu.HBM)
            for x in (
                latents,
                rotary_rows,
                latent_gain.reshape(1, LATENT),
                key_up.reshape(2 * LATENT, PART),
                value_up.reshape(2 * LATENT, PART),
            )
        )
    )
    keys, values = pl.pallas_call(
        write_kernel,
        out_shape=(
            jax.ShapeDtypeStruct((2, PART + ROTARY, SPAN * TILE), jnp.bfloat16),
            jax.ShapeDtypeStruct((SPAN * TILE * 2, PART), jnp.bfloat16),
        ),
        in_specs=[anywhere, anywhere],
        out_specs=(anywhere, anywhere),
        scratch_shapes=[pltpu.SemaphoreType.DMA((2,))],
        compiler_params=pltpu.CompilerParams(vmem_limit_bytes=24 * 2**20),
    )(kst, vst)
    return keys[None], values.reshape(1, SPAN * TILE, 2, PART)


def solution(mesh):
    return jax.shard_map(
        shards,
        mesh=mesh,
        in_specs=(
            P("trial", ("span", "heads"), None),
            P("trial", ("span", "heads"), None),
            P(),
            P("trial", "heads", None),
            P("trial", "heads", None),
        ),
        out_specs=(
            P(("trial", "span"), "heads", None, None),
            P(("trial", "span"), None, "heads", None),
        ),
        check_vma=False,
    )
```

time: 79.3 us -> 69.3 us (0.87); the launches traced: 79.2 us -> 67.9 us
  Pallas kernels: 73.1 us -> 67.3 us
  local copies, waits for them, and re-layouts: 5.38 us -> 0 us
    pallas_call x1 -> x2, Pallas kernels: 73.1 us -> 67.3 us  [the longest x1 65 us: shards(): pl.pallas_call(gather_kernel, out_shape=(pltpu.VMEM((SPAN, 2, PART + ROTA...]
    unnamed x4 -> x0, local copies, waits for them, and re-layouts: 5.38 us -> none
where the time goes in v2:
time: 69.3 us; the launch traced here: 67.9 us
  Pallas kernels  67.3 us (97%)
    pallas_call x1, Pallas kernels, shards(): pl.pallas_call(gather_kernel, out_shape=(pltpu.VMEM((SPAN, 2, PART + ROTA...  65 us
    pallas_call x1, Pallas kernels, shards(): pl.pallas_call(write_kernel, out_shape=(jax.ShapeDtypeStruct((2, PART + R...  2.34 us

profile of v2, /device:TPU:6, one launch (start us, length us, event | category | flops | bytes accessed | tf_op | source)
XLA Modules:
  0.0 67.9 jit_solution(3513539803427811869)
XLA Ops:
  0.6 65.0 %shard_map.68 = (bf16[16,2,192,256]{3,2,1,0:T(8,128)(2,1)S(1)}, bf16[16,512,128]{2,1,0:T(8,128)(2,1)S(1)}) custom-call(bf16[16,32,512]{2,1,0:T(8,128)(2,1)} %lat_hbm.1, bf16[16,32,64]{2,1,0:T(8,128)(2,1)} %rot_hbm.1, f32[1,512]{1,0:T(1,128)} %bitcast.7, bf16[1024,128]{1,0:T(8,128)(2,1)} %bitcast.5, bf16[1024,128]{1,0:T(8,128)(2,1)} %bitcast.6), custom_call_target="tpu_custom_call" | custom-call | tf_op jit(solution)/shard_map/pallas_call | solution.py:212
  65.6 2.3 %shard_map.69 = (bf16[2,192,4096]{2,1,0:T(8,128)(2,1)}, bf16[8192,128]{1,0:T(8,128)(2,1)}) custom-call(bf16[16,2,192,256]{3,2,1,0:T(8,128)(2,1)S(1)} %get-tuple-element.6.kst, bf16[16,512,128]{2,1,0:T(8,128)(2,1)S(1)} %get-tuple-element.7.vst), custom_call_target="tpu_custom_call" | custom-call | tf_op jit(solution)/shard_map/pallas_call | solution.py:256

commit v3 on v2

--- a/solution.py
+++ b/solution.py
@@ -13,7 +13,8 @@
 ROTARY = 64
 PART = 128
 CHUNK = 144
-GROUP = 8
+MOVED = 4
+WEIGH_AT = 40
 TILE = RING * ROWS
 
 
@@ -37,38 +38,28 @@
     return ((y + 8 - dy) % 8) * 2 + other
 
 
+KINDS = ("up", "down", "finish")
+ORDER = (
+    68, 4, 72, 8, 65, 1, 76, 12, 80, 16, 84, 20, 69, 5, 88, 24, 73, 9, 92, 28, 66, 2, 77, 13, 96, 32, 81, 17,
+    100, 36, 85, 21, 104, 40, 89, 25, 108, 44, 93, 29, 112, 48, 97, 33, 116, 52, 101, 37, 120, 56, 105, 41,
+    124, 60, 109, 45, 70, 6, 113, 49, 74, 10, 117, 53, 78, 14, 121, 57, 82, 18, 125, 61, 86, 22, 90, 26, 94,
+    30, 98, 34, 102, 38, 106, 42, 110, 46, 114, 50, 118, 54, 122, 58, 126, 62, 99, 3, 83, 103, 7, 87, 107, 11,
+    91, 111, 15, 95, 115, 19, 119, 23, 123, 27, 127, 31, 128, 132, 136, 140, 144, 148, 152, 156,
+)
+
+
 def schedule():
-    half = GROUP // 2
-    order = [m // 2 + half * (m % 2) for m in range(GROUP)]
-    events, owed = [], []
-    for first in range(0, SPAN, GROUP):
-        for step in range(4):
-            for m in range(GROUP):
-                if step < 3 or m < half:
-                    events.append(("up", first + m, step))
-                if step < 3 or m >= half:
-                    events.append(("down", first + m, step))
-            events += [("finish", j, 0) for j in owed[:half]]
-            owed = owed[half:]
-        owed = [first + m for m in order]
-    return events + [("finish", j, 0) for j in owed]
+    return [(KINDS[code // 64], code // 4 % 16, code % 4) for code in ORDER]
 
 
 def gather_kernel(
     lat_hbm, rot_hbm, gain_hbm, wk_hbm, wv_hbm,
     kst, vst,
     own_lat, lat, rot, gain, wk_pairs, wv_pairs, wide, wk, wv, ready, held, vwide,
-    in_sem, swap_send, swap_recv, up_send, up_recv, down_send, down_recv,
+    in_sem, swap_send, swap_recv, up_send, up_recv, down_send, down_recv, moved_send, known,
 ):
     span, z = lax.axis_index("span"), lax.axis_index("heads")
     up, down = (z + 1) % RING, (z + RING - 1) % RING
-    half = GROUP // 2
-
-    barrier = pltpu.get_barrier_semaphore()
-    for peer in (up, down):
-        pl.semaphore_signal(barrier, inc=1, device_id={"heads": peer}, device_id_type=MESH)
-    for j in range(1, SPAN):
-        pl.semaphore_signal(barrier, inc=1, device_id={"span": target_of(j, span)}, device_id_type=MESH)
 
     loads = [
         pltpu.make_async_copy(source, into, in_sem.at[n])
@@ -79,8 +70,26 @@
             )
         )
     ]
-    for load in loads:
+    for load in loads[:3]:
         load.start()
+
+    y, core = span // 2, span % 2
+    beside = [2 * ((y + step) % 8) for step in (1, 7)]
+    barrier = pltpu.get_barrier_semaphore()
+    for peer in (up, down):
+        pl.semaphore_signal(barrier, inc=1, device_id={"heads": peer}, device_id_type=MESH)
+    for peer in (2 * y + 1 - core, *(first + c for first in beside for c in range(2))):
+        pl.semaphore_signal(barrier, inc=1, device_id={"span": peer}, device_id_type=MESH)
+
+    for load in loads[3:]:
+        load.start()
+
+    def tell(level):
+        for first in beside:
+            pl.semaphore_signal(known.at[level], inc=1, device_id={"span": first + core}, device_id_type=MESH)
+
+    def hear(level):
+        pl.semaphore_wait(known.at[level], 2)
 
     def packed(x, r, store):
         x = x.astype(jnp.float32)
@@ -100,12 +109,12 @@
             device_id_type=MESH,
         )
 
-    def hop(way, j, k):
+    def hop(way, j, k, sent=None):
         owner = (z + RING - k) % RING if way == "up" else (z + k) % RING
         return pltpu.make_async_remote_copy(
             src_ref=held.at[j, owner],
             dst_ref=held.at[j, owner],
-            send_sem=up_send if way == "up" else down_send,
+            send_sem=(up_send if way == "up" else down_send) if sent is None else sent,
             recv_sem=(up_recv if way == "up" else down_recv).at[j, k],
             device_id={"heads": up if way == "up" else down},
             device_id_type=MESH,
@@ -144,13 +153,24 @@
     packed(own_lat[...], rot[span], store_own)
     loads[3].wait()
     prepare(1)
-    pl.semaphore_wait(barrier, SPAN - 1 + 2)
+    pl.semaphore_wait(barrier, 7)
+    tell(0)
     hop("up", 0, 0).start()
     hop("down", 0, 0).start()
-    for j in range(1, SPAN):
-        if j + 1 < SPAN:
-            prepare(j + 1)
-        swap(j).start()
+    swapped = set()
+
+    def start_swaps(upto):
+        for j in range(1, upto + 1):
+            if j not in swapped:
+                swapped.add(j)
+                if j in (6, 10, 14):
+                    level = j // 4 - 1
+                    hear(level)
+                    if level < 2:
+                        tell(level + 1)
+                if j + 1 < SPAN:
+                    prepare(j + 1)
+                swap(j).start()
 
     arrived = set()
 
@@ -162,36 +182,63 @@
             else:
                 hop(kind, j, k).wait_recv()
 
-    weighed = False
-    for kind, j, k in schedule():
+    start_swaps(5)
+    def weigh():
+        for load in loads[4:]:
+            load.wait()
+        wide[...] = wk_pairs[...].astype(jnp.float32)
+        for h in range(2):
+            wk[pl.ds(h * PART, PART), :] = wide[pl.ds(h, LATENT, stride=2), :].T.astype(jnp.bfloat16)
+        wide[...] = wv_pairs[...].astype(jnp.float32)
+        for h in range(2):
+            wv[:, pl.ds(h * PART, PART)] = wide[pl.ds(h, LATENT, stride=2), :].astype(jnp.bfloat16)
+
+    for number, (kind, j, k) in enumerate(schedule()):
+        if number == WEIGH_AT:
+            weigh()
         if kind == "finish":
-            if not weighed:
-                weighed = True
-                for load in loads[4:]:
-                    load.wait()
-                wide[...] = wk_pairs[...].astype(jnp.float32)
-                for h in range(2):
-                    wk[pl.ds(h * PART, PART), :] = wide[pl.ds(h, LATENT, stride=2), :].T.astype(jnp.bfloat16)
-                wide[...] = wv_pairs[...].astype(jnp.float32)
-                for h in range(2):
-                    wv[:, pl.ds(h * PART, PART)] = wide[pl.ds(h, LATENT, stride=2), :].astype(jnp.bfloat16)
-            last_up = 3 if j % GROUP < half else 2
-            arrive("up", j, last_up)
-            arrive("down", j, 5 - last_up)
-            finish(j)
+            pair = (j, j + SPAN // 2)
+            for one in pair:
+                by_up = one < SPAN // 2
+                if by_up and one >= SPAN // 2 - MOVED:
+                    pl.when(z == 0)(hop("down", one, 3).wait_recv)
+                    pl.when(z != 0)(hop("up", one, 3).wait_recv)
+                else:
+                    arrive("up" if by_up else "down", one, 3)
+                arrive("down" if by_up else "up", one, 2)
+            for one in pair:
+                finish(one)
         elif (j, k) != (0, 0):
             if k > 0:
                 arrive(kind, j, k - 1)
             else:
                 arrive("swap", j, 0)
-            hop(kind, j, k).start()
+            if k < 3 or not SPAN // 2 - MOVED <= j < SPAN // 2:
+                hop(kind, j, k).start()
+            elif kind == "up":
+                pl.when(z < RING - 1)(hop(kind, j, k).start)
+            else:
+                pl.when(z == 1)(hop(kind, j, k, moved_send).start)
+            if kind == "down" and k == 0:
+                start_swaps(min(SPAN - 1, 5 + 4 * j))
 
     def all_of(ref, sem):
         pltpu.make_async_copy(ref, ref, sem).wait()
 
     all_of(ready.at[pl.ds(1, SPAN - 1)], swap_send)
-    all_of(held.at[pl.ds(0, 7)], up_send)
     all_of(held.at[pl.ds(0, 7)], down_send)
+
+    @pl.when(z < RING - 1)
+    def _():
+        all_of(held.at[pl.ds(0, 7)], up_send)
+
+    @pl.when(z == RING - 1)
+    def _():
+        all_of(held.at[pl.ds(0, 13), pl.ds(0, 4)], up_send)
+
+    @pl.when(z == 1)
+    def _():
+        all_of(held.at[0, pl.ds(0, MOVED)], moved_send)
 
 
 def write_kernel(kst, vst, keys_hbm, values_hbm, sem):
@@ -237,6 +284,8 @@
             pltpu.SemaphoreType.DMA((SPAN, 4)),
             pltpu.SemaphoreType.DMA,
             pltpu.SemaphoreType.DMA((SPAN, 4)),
+            pltpu.SemaphoreType.DMA,
+            pltpu.SemaphoreType.REGULAR((3,)),
         ],
         compiler_params=pltpu.CompilerParams(
             collective_id=0, has_side_effects=True, vmem_limit_bytes=24 * 2**20

time: 69.3 us -> 64.8 us (0.935); the launches traced: 67.9 us -> 64.5 us
  Pallas kernels: 67.3 us -> 63.9 us
    pallas_call x1, Pallas kernels: 65 us -> 61.5 us  [shards(): pl.pallas_call(gather_kernel, out_shape=(pltpu.VMEM((SPAN, 2, PART + ROTA...]
where the time goes in v3:
time: 64.8 us; the launch traced here: 64.5 us
  Pallas kernels  63.9 us (99%)
    pallas_call x1, Pallas kernels, shards(): pl.pallas_call(gather_kernel, out_shape=(pltpu.VMEM((SPAN, 2, PART + ROTA...  61.5 us
    pallas_call x1, Pallas kernels, shards(): pl.pallas_call(write_kernel, out_shape=(jax.ShapeDtypeStruct((2, PART + R...  2.34 us

profile of v3, /device:TPU:6, one launch (start us, length us, event | category | flops | bytes accessed | tf_op | source)
XLA Modules:
  0.0 64.5 jit_solution(7485092724341892158)
XLA Ops:
  0.6 61.5 %shard_map.68 = (bf16[16,2,192,256]{3,2,1,0:T(8,128)(2,1)S(1)}, bf16[16,512,128]{2,1,0:T(8,128)(2,1)S(1)}) custom-call(bf16[16,32,512]{2,1,0:T(8,128)(2,1)} %lat_hbm.1, bf16[16,32,64]{2,1,0:T(8,128)(2,1)} %rot_hbm.1, f32[1,512]{1,0:T(1,128)} %bitcast.7, bf16[1024,128]{1,0:T(8,128)(2,1)} %bitcast.5, bf16[1024,128]{1,0:T(8,128)(2,1)} %bitcast.6), custom_call_target="tpu_custom_call" | custom-call | tf_op jit(solution)/shard_map/pallas_call | solution.py:259
  62.1 2.3 %shard_map.69 = (bf16[2,192,4096]{2,1,0:T(8,128)(2,1)}, bf16[8192,128]{1,0:T(8,128)(2,1)}) custom-call(bf16[16,2,192,256]{3,2,1,0:T(8,128)(2,1)S(1)} %get-tuple-element.6.kst, bf16[16,512,128]{2,1,0:T(8,128)(2,1)S(1)} %get-tuple-element.7.vst), custom_call_target="tpu_custom_call" | custom-call | tf_op jit(solution)/shard_map/pallas_call | solution.py:305

commit v4 on v3

--- a/solution.py
+++ b/solution.py
@@ -13,6 +13,7 @@
 ROTARY = 64
 PART = 128
 CHUNK = 144
+LAST = (7, 15)
 MOVED = 4
 WEIGH_AT = 40
 TILE = RING * ROWS
@@ -40,11 +41,11 @@
 
 KINDS = ("up", "down", "finish")
 ORDER = (
-    68, 4, 72, 8, 65, 1, 76, 12, 80, 16, 84, 20, 69, 5, 88, 24, 73, 9, 92, 28, 66, 2, 77, 13, 96, 32, 81, 17,
-    100, 36, 85, 21, 104, 40, 89, 25, 108, 44, 93, 29, 112, 48, 97, 33, 116, 52, 101, 37, 120, 56, 105, 41,
-    124, 60, 109, 45, 70, 6, 113, 49, 74, 10, 117, 53, 78, 14, 121, 57, 82, 18, 125, 61, 86, 22, 90, 26, 94,
-    30, 98, 34, 102, 38, 106, 42, 110, 46, 114, 50, 118, 54, 122, 58, 126, 62, 99, 3, 83, 103, 7, 87, 107, 11,
-    91, 111, 15, 95, 115, 19, 119, 23, 123, 27, 127, 31, 128, 132, 136, 140, 144, 148, 152, 156,
+    68, 4, 72, 8, 65, 1, 76, 12, 80, 16, 84, 20, 69, 5, 88, 24, 73, 9, 92, 28, 96, 32, 77, 13, 100, 36, 104,
+    40, 81, 17, 108, 44, 112, 48, 85, 21, 116, 52, 120, 56, 89, 25, 124, 60, 93, 29, 97, 33, 101, 37, 105, 41,
+    109, 45, 113, 49, 117, 53, 121, 57, 125, 61, 66, 2, 70, 6, 74, 10, 78, 14, 82, 18, 86, 22, 90, 26, 94, 30,
+    98, 34, 102, 38, 106, 42, 110, 46, 114, 50, 118, 54, 122, 58, 126, 62, 99, 3, 83, 103, 7, 87, 107, 11, 91,
+    111, 15, 95, 115, 19, 119, 23, 123, 27, 127, 31, 128, 132, 136, 140, 144, 148, 152, 156,
 )
 
 
@@ -52,10 +53,28 @@
     return [(KINDS[code // 64], code // 4 % 16, code % 4) for code in ORDER]
 
 
+def expand(chunk, wk, wv, vwide, keys_out, values_out):
+    rows = jnp.concatenate(
+        [chunk[:, pl.ds(q * ROWS, ROWS), :].reshape(TILE, 128) for q in range(4)], axis=1
+    )
+    keys = lax.dot_general(
+        wk[...], rows, (((1,), (1,)), ((), ())), preferred_element_type=jnp.float32
+    ).astype(jnp.bfloat16)
+    turned = chunk[:, pl.ds(4 * ROWS, 16), :].astype(jnp.float32)
+    turned = jnp.concatenate([turned[:, :, :ROTARY], turned[:, :, ROTARY:]], axis=1)
+    turned = turned.reshape(TILE, ROTARY).T.astype(jnp.bfloat16)
+    values = jnp.dot(rows, wv[...], preferred_element_type=jnp.float32)
+    for h in range(2):
+        keys_out[h, pl.ds(0, PART), :] = keys[h * PART : (h + 1) * PART]
+        keys_out[h, pl.ds(PART, ROTARY), :] = turned
+        vwide[pl.ds(h, TILE, stride=2), :] = values[:, h * PART : (h + 1) * PART]
+    values_out[...] = vwide[...].astype(jnp.bfloat16)
+
+
 def gather_kernel(
     lat_hbm, rot_hbm, gain_hbm, wk_hbm, wv_hbm,
-    kst, vst,
-    own_lat, lat, rot, gain, wk_pairs, wv_pairs, wide, wk, wv, ready, held, vwide,
+    kst, vst, held, wk, wv,
+    own_lat, lat, rot, gain, wk_pairs, wv_pairs, wide, ready, vwide,
     in_sem, swap_send, swap_recv, up_send, up_recv, down_send, down_recv, moved_send, known,
 ):
     span, z = lax.axis_index("span"), lax.axis_index("heads")
@@ -121,21 +140,7 @@
         )
 
     def finish(j):
-        rows = jnp.concatenate(
-            [held[j, :, pl.ds(q * ROWS, ROWS), :].reshape(TILE, 128) for q in range(4)], axis=1
-        )
-        keys = lax.dot_general(
-            wk[...], rows, (((1,), (1,)), ((), ())), preferred_element_type=jnp.float32
-        ).astype(jnp.bfloat16)
-        turned = held[j, :, pl.ds(4 * ROWS, 16), :].astype(jnp.float32)
-        turned = jnp.concatenate([turned[:, :, :ROTARY], turned[:, :, ROTARY:]], axis=1)
-        turned = turned.reshape(TILE, ROTARY).T.astype(jnp.bfloat16)
-        values = jnp.dot(rows, wv[...], preferred_element_type=jnp.float32)
-        for h in range(2):
-            kst[j, h, pl.ds(0, PART), :] = keys[h * PART : (h + 1) * PART]
-            kst[j, h, pl.ds(PART, ROTARY), :] = turned
-            vwide[pl.ds(h, TILE, stride=2), :] = values[:, h * PART : (h + 1) * PART]
-        vst[j] = vwide[...].astype(jnp.bfloat16)
+        expand(held.at[j], wk, wv, vwide, kst.at[j], vst.at[j])
 
     def store_own(at, x):
         held[0, z, at, :] = x
@@ -206,8 +211,9 @@
                 else:
                     arrive("up" if by_up else "down", one, 3)
                 arrive("down" if by_up else "up", one, 2)
-            for one in pair:
-                finish(one)
+            if pair != LAST:
+                for one in pair:
+                    finish(one)
         elif (j, k) != (0, 0):
             if k > 0:
                 arrive(kind, j, k - 1)
@@ -241,14 +247,23 @@
         all_of(held.at[0, pl.ds(0, MOVED)], moved_send)
 
 
-def write_kernel(kst, vst, keys_hbm, values_hbm, sem):
+def write_kernel(kst, vst, held, wk, wv, keys_hbm, values_hbm, vwide, last_keys, last_values, sem):
     span = lax.axis_index("span")
+
+    def write(j, keys, values):
+        at = source_of(j, span) * TILE
+        pltpu.make_async_copy(keys, keys_hbm.at[:, :, pl.ds(pl.multiple_of(at, TILE), TILE)], sem.at[0]).start()
+        pltpu.make_async_copy(
+            values, values_hbm.at[pl.ds(pl.multiple_of(2 * at, 2 * TILE), 2 * TILE), :], sem.at[1]
+        ).start()
+
     for j in range(SPAN):
-        at = source_of(j, span) * TILE
-        pltpu.make_async_copy(kst.at[j], keys_hbm.at[:, :, pl.ds(pl.multiple_of(at, TILE), TILE)], sem.at[0]).start()
-        pltpu.make_async_copy(
-            vst.at[j], values_hbm.at[pl.ds(pl.multiple_of(2 * at, 2 * TILE), 2 * TILE), :], sem.at[1]
-        ).start()
+        if j not in LAST:
+            write(j, kst.at[j], vst.at[j])
+    for n, j in enumerate(LAST):
+        expand(held.at[j], wk, wv, vwide.at[n], last_keys.at[n], last_values.at[n])
+    for n, j in enumerate(LAST):
+        write(j, last_keys.at[n], last_values.at[n])
     pltpu.make_async_copy(kst, kst, sem.at[0]).wait()
     pltpu.make_async_copy(vst, vst, sem.at[1]).wait()
 
@@ -256,14 +271,17 @@
 def shards(latents, rotary_rows, latent_gain, key_up, value_up):
     anywhere = pl.BlockSpec(memory_space=pl.ANY)
     here = pl.BlockSpec(memory_space=pltpu.VMEM)
-    kst, vst = pl.pallas_call(
+    gathered = pl.pallas_call(
         gather_kernel,
         out_shape=(
             pltpu.VMEM((SPAN, 2, PART + ROTARY, TILE), jnp.bfloat16),
             pltpu.VMEM((SPAN, 2 * TILE, PART), jnp.bfloat16),
+            pltpu.VMEM((SPAN, RING, CHUNK, 128), jnp.bfloat16),
+            pltpu.VMEM((2 * PART, LATENT), jnp.bfloat16),
+            pltpu.VMEM((LATENT, 2 * PART), jnp.bfloat16),
         ),
         in_specs=[pl.BlockSpec(memory_space=pltpu.HBM)] * 5,
-        out_specs=(here, here),
+        out_specs=(here,) * 5,
         scratch_shapes=[
             pltpu.VMEM((ROWS, LATENT), jnp.bfloat16),
             pltpu.VMEM((SPAN, ROWS, LATENT), jnp.bfloat16),
@@ -272,10 +290,7 @@
             pltpu.VMEM((2 * LATENT, PART), jnp.bfloat16),
             pltpu.VMEM((2 * LATENT, PART), jnp.bfloat16),
             pltpu.VMEM((2 * LATENT, PART), jnp.float32),
-            pltpu.VMEM((2 * PART, LATENT), jnp.bfloat16),
-            pltpu.VMEM((LATENT, 2 * PART), jnp.bfloat16),
             pltpu.VMEM((SPAN, CHUNK, 128), jnp.bfloat16),
-            pltpu.VMEM((SPAN, RING, CHUNK, 128), jnp.bfloat16),
             pltpu.VMEM((2 * TILE, PART), jnp.float32),
             pltpu.SemaphoreType.DMA((6,)),
             pltpu.SemaphoreType.DMA,
@@ -308,11 +323,16 @@
             jax.ShapeDtypeStruct((2, PART + ROTARY, SPAN * TILE), jnp.bfloat16),
             jax.ShapeDtypeStruct((SPAN * TILE * 2, PART), jnp.bfloat16),
         ),
-        in_specs=[anywhere, anywhere],
+        in_specs=[here] * 5,
         out_specs=(anywhere, anywhere),
-        scratch_shapes=[pltpu.SemaphoreType.DMA((2,))],
+        scratch_shapes=[
+            pltpu.VMEM((2, 2 * TILE, PART), jnp.float32),
+            pltpu.VMEM((2, 2, PART + ROTARY, TILE), jnp.bfloat16),
+            pltpu.VMEM((2, 2 * TILE, PART), jnp.bfloat16),
+            pltpu.SemaphoreType.DMA((2,)),
+        ],
         compiler_params=pltpu.CompilerParams(vmem_limit_bytes=24 * 2**20),
-    )(kst, vst)
+    )(*(pltpu.with_memory_space_constraint(x, pltpu.VMEM) for x in gathered))
     return keys[None], values.reshape(1, SPAN * TILE, 2, PART)
 
 

time: 64.8 us -> 64.6 us (level)
  no operation moved by 1% of the time
where the time goes in v4:
time: 64.6 us; the launch traced here: 64.3 us
  Pallas kernels  63.7 us (99%)
    pallas_call x1, Pallas kernels, shards(): pl.pallas_call(gather_kernel, out_shape=(pltpu.VMEM((SPAN, 2, PART + ROTA...  61 us
    pallas_call x1, Pallas kernels, shards(): pl.pallas_call(write_kernel, out_shape=(jax.ShapeDtypeStruct((2, PART + R...  2.68 us

profile of v4, /device:TPU:6, one launch (start us, length us, event | category | flops | bytes accessed | tf_op | source)
XLA Modules:
  0.0 64.3 jit_solution(7351371069998885845)
XLA Ops:
  0.6 61.0 %shard_map.68 = (bf16[16,2,192,256]{3,2,1,0:T(8,128)(2,1)S(1)}, bf16[16,512,128]{2,1,0:T(8,128)(2,1)S(1)}, bf16[16,8,144,128]{3,2,1,0:T(8,128)(2,1)S(1)}, bf16[2...) custom-call(bf16[16,32,512]{2,1,0:T(8,128)(2,1)} %lat_hbm.1, bf16[16,32,64]{2,1,0:T(8,128)(2,1)} %rot_hbm.1, f32[1,512]{1,0:T(1,128)} %bitcast.7, ...), custom_call_target="tpu_custom_call" | custom-call | tf_op jit(solution)/shard_map/pallas_call | solution.py:274
  61.6 2.7 %shard_map.69 = (bf16[2,192,4096]{2,1,0:T(8,128)(2,1)}, bf16[8192,128]{1,0:T(8,128)(2,1)}) custom-call(bf16[16,2,192,256]{3,2,1,0:T(8,128)(2,1)S(1)} %get-tuple-element.9.kst, bf16[16,512,128]{2,1,0:T(8,128)(2,1)S(1)} %get-tuple-element.10.vst, bf16[16,8,144,128]{3,2,1,0:T(8,128)(2,1)S(1)} %get-tuple-element.11.held, ...), custom_call_target="tpu_custom_call" | custom-call | tf_op jit(solution)/shard_map/pallas_call | solution.py:320
